TPU v7x, 32 devices: a whole 2x2x4 slice. The times are simulated.
32 devices in a mesh: inl: 4 (over z), xln: 8 (over y, x, core).
Axes of the slice: x: 2, y: 2, z: 4, core: 2. Of those that a mesh axis runs over, the one named last changes fastest.
Arguments:
- noisy: float32 [128, 256, 512], P('inl', 'xln'), may hold values from -6 to 6
- bound: float32 [128, 256, 512], P('inl', 'xln'), may hold values from 0.05 to 0.5
Outputs:
- denoised: float32 [128, 256, 512], P('inl', 'xln')
- dual: float32 [3, 128, 256, 512], P(None, 'inl', 'xln')
- norms: float32 [2, 2], replicated
All inputs are finite; a program needn't handle non-finite values.
Results may differ from a plain program's by a relative error of at most 0.0001.
Values sent between devices are 32-bit elements; how exact they have to be, the bound alone decides.
A program may use at most 64 MiB of HBM per device.

v0:
```python
import jax
import jax.numpy as jnp
from jax import lax
from jax.sharding import PartitionSpec as P

ITERS = 2


SIGMA = 0.28
TAU = 0.28


def passed_along(value, axis, steps):
    count = lax.axis_size(axis)
    first, last = (max(0, -steps), min(count, count - steps))
    return lax.ppermute(value, axis, [(source, source + steps) for source in range(first, last)])


def depth_forward(field):
    return jnp.concatenate(
        [field[:, :, 1:] - field[:, :, :-1], jnp.zeros_like(field[:, :, :1])], axis=2
    )


def depth_backward(field):
    return field - jnp.concatenate([jnp.zeros_like(field[:, :, :1]), field[:, :, :-1]], axis=2)


def finish(sums_list):
    return jnp.sqrt(lax.psum(jnp.stack(sums_list), ("inl", "xln")))


def record(primal_sum, dual_sum, sums_list):
    sums_list.append(jnp.stack([primal_sum, dual_sum]))


def per_device(noisy, bound):
    sums_list = []
    inl_flag = (lax.axis_index("inl") < lax.axis_size("inl") - 1).astype(jnp.float32)
    xln_flag = (lax.axis_index("xln") < lax.axis_size("xln") - 1).astype(jnp.float32)
    primal = noisy
    smooth = noisy
    dual_i = jnp.zeros_like(noisy)
    dual_x = jnp.zeros_like(noisy)
    dual_z = jnp.zeros_like(noisy)
    for step in range(ITERS):
        next_i = passed_along(smooth[0:1], "inl", -1)
        next_x = passed_along(smooth[:, 0:1], "xln", -1)
        grad_i = jnp.concatenate(
            [smooth[1:] - smooth[:-1], (next_i - smooth[-1:]) * inl_flag], axis=0
        )
        grad_x = jnp.concatenate(
            [smooth[:, 1:] - smooth[:, :-1], (next_x - smooth[:, -1:]) * xln_flag], axis=1
        )
        fresh_i = jnp.clip(dual_i + SIGMA * grad_i, -bound, bound)
        fresh_x = jnp.clip(dual_x + SIGMA * grad_x, -bound, bound)
        fresh_z = jnp.clip(dual_z + SIGMA * depth_forward(smooth), -bound, bound)
        prev_i = passed_along(fresh_i[-1:], "inl", 1)
        prev_x = passed_along(fresh_x[:, -1:], "xln", 1)
        diverge = fresh_i - jnp.concatenate([prev_i, fresh_i[:-1]], axis=0)
        diverge = diverge + (fresh_x - jnp.concatenate([prev_x, fresh_x[:, :-1]], axis=1))
        diverge = diverge + depth_backward(fresh_z)
        updated = (primal + TAU * diverge + TAU * noisy) / (1.0 + TAU)
        primal_sum = jnp.sum((updated - primal) ** 2)
        dual_sum = (
            jnp.sum((fresh_i - dual_i) ** 2)
            + jnp.sum((fresh_x - dual_x) ** 2)
            + jnp.sum((fresh_z - dual_z) ** 2)
        )
        record(primal_sum, dual_sum, sums_list)
        smooth = 2.0 * updated - primal
        primal = updated
        dual_i, dual_x, dual_z = (fresh_i, fresh_x, fresh_z)
    norms = finish(sums_list)
    return (primal, jnp.stack([dual_i, dual_x, dual_z]), norms)


def solution(mesh):
    in_specs = (P("inl", "xln", None), P("inl", "xln", None))
    out_specs = (P("inl", "xln", None), P(None, "inl", "xln", None), P())
    return jax.shard_map(
        per_device, mesh=mesh, in_specs=in_specs, out_specs=out_specs, check_vma=False
    )
```

profile of v0, /device:TPU:0, one launch (start us, length us, event | category | flops | bytes accessed | tf_op | source)
XLA Modules:
  0.0 110.8 jit_solution(10471086511929388984)
XLA Ops:
  0.6 0.8 slice.92
  1.5 1.3 %collective-permute-start = (f32[1,32,512]{2,1,0:T(8,128)S(1)}, f32[1,32,512]{2,1,0:T(8,128)S(1)}, u32[]{:S(2)}, u32[]{:S(2)}) collective-permute-start(f32[1,32,512]{2,1,0:T(8,128)S(1)} %slice.92), channel_id=1, source_target_pairs={{8,0},{16,8},{24,16},{9,1},{17,9},{25,17},{10,2},{18,10},{26,18},{... | collective-permute-start | bytes 196616 | tf_op jit(solution)/shard_map/ppermute | solution.py:16
  2.8 1.1 slice.98
  3.8 0.0 copy-start
  3.9 1.4 %collective-permute-start.2 = (f32[32,1,512]{2,1,0:T(1,128)S(1)}, f32[32,1,512]{2,1,0:T(1,128)S(1)}, u32[]{:S(2)}, u32[]{:S(2)}) collective-permute-start(f32[32,1,512]{2,1,0:T(1,128)S(1)} %slice.98), channel_id=1, source_target_pairs={{1,0},{2,1},{3,2},{4,3},{5,4},{6,5},{7,6},{9,8},{10,9},{11,10},{12... | collective-permute-start | bytes 196616 | tf_op jit(solution)/shard_map/ppermute | solution.py:16
  5.3 4.1 %slice_subtract_fusion.3 = f32[32,31,512]{2,1,0:T(8,128)} fusion(f32[32,32,512]{2,1,0:T(8,128)} %param.2), kind=kLoop, calls=%fused_computation.44 | loop fusion | flops 507904 | bytes 6094848 | tf_op jit(solution)/shard_map/sub | solution.py:53
  9.4 0.0 copy-done
  9.4 2.0 %slice_subtract_fusion.2 = f32[32,32,511]{2,1,0:T(8,128)} fusion(f32[32,32,512]{2,1,0:T(8,128)S(1)} %copy-done), kind=kLoop, calls=%fused_computation.43 | loop fusion | flops 523264 | bytes 6279168 | tf_op jit(solution)/shard_map/sub | solution.py:21
  11.3 1.7 %slice_subtract_fusion.5 = f32[31,32,512]{2,1,0:T(8,128)} fusion(f32[32,32,512]{2,1,0:T(8,128)S(1)} %copy-done), kind=kLoop, calls=%fused_computation.46 | loop fusion | flops 507904 | bytes 6094848 | tf_op jit(solution)/shard_map/sub | solution.py:50
  13.0 0.0 collective-permute-done
  13.0 0.0 collective-permute-done.2
  13.0 0.1 subtract_multiply_fusion
  13.1 4.5 %fusion.1 = (f32[32,32,512]{2,1,0:T(8,128)S(1)}, f32[32,32,512]{2,1,0:T(8,128)S(1)}, f32[32,32,512]{2,1,0:T(8,128)S(1)}) fusion(f32[32,32,512]{2,1,0:T(8,128)} %param.3, f32[1,32,512]{2,1,0:T(8,128)S(1)} %subtract_multiply_fusion.1, f32[31,32,512]{2,1,0:T(8,128)} %slice_subtract_fusion.5, f32[32,32,511]{2,1,0:T(8,128)} %slice_subtract_fusion.2, ...), kind=kLoop, calls=%fused_computation.5 | loop fusion | flops 6291456 | bytes 14675968 | tf_op jit(solution)/shard_map/jit(clip)/min | solution.py:55
  17.7 0.1 slice.122
  17.7 3.0 %collective-permute-start.3 = (f32[32,1,512]{2,1,0:T(1,128)S(1)}, f32[32,1,512]{2,1,0:T(1,128)S(1)}, u32[]{:S(2)}, u32[]{:S(2)}) collective-permute-start(f32[32,1,512]{2,1,0:T(1,128)S(1)} %slice.122), channel_id=1, source_target_pairs={{0,1},{1,2},{2,3},{3,4},{4,5},{5,6},{6,7},{8,9},{9,10},{10,11},{11... | collective-permute-start | bytes 196616 | tf_op jit(solution)/shard_map/ppermute | solution.py:16
  20.8 5.6 %collective-permute-start.1 = (f32[1,32,512]{2,1,0:T(8,128)S(1)}, f32[1,32,512]{2,1,0:T(8,128)S(1)}, u32[]{:S(2)}, u32[]{:S(2)}) collective-permute-start(f32[1,32,512]{2,1,0:T(8,128)S(1)} %slice.120), channel_id=1, source_target_pairs={{0,8},{8,16},{16,24},{1,9},{9,17},{17,25},{2,10},{10,18},{18,26},{... | collective-permute-start | bytes 196616 | tf_op jit(solution)/shard_map/ppermute | solution.py:16
  26.4 0.3 slice.121
  26.6 0.0 collective-permute-done.3
  26.6 1.6 %collective-permute-done.1 = f32[1,32,512]{2,1,0:T(8,128)S(1)} collective-permute-done((f32[1,32,512]{2,1,0:T(8,128)S(1)}, f32[1,32,512]{2,1,0:T(8,128)S(1)}, u32[]{:S(2)}, u32[]{:S(2)}) %collective-permute-start.1) | collective-permute-done | bytes 65568 | tf_op jit(solution)/shard_map/ppermute | solution.py:16
  28.3 3.5 %multiply_subtract_fusion = (f32[32,32,512]{2,1,0:T(8,128)S(1)}, f32[32,32,512]{2,1,0:T(8,128)}) fusion(f32[32,32,512]{2,1,0:T(8,128)S(1)} %copy-done, f32[32,32,512]{2,1,0:T(8,128)S(1)} %get-tuple-element.24, f32[32,32,511]{2,1,0:T(8,128)S(1)} %bitcast.18, f32[32,32,512]{2,1,0:T(8,128)S(1)} %get-tuple-element.25, f32[32,31,512]{2,1,0:T(8,128)S(1)} %bitcast.15, ...), kind=kLoop, calls=%fused_computation.41 | loop fusion | flops 6815744 | bytes 18870272 | tf_op jit(solution)/shard_map/sub | solution.py:71
  31.7 0.3 slice_subtract_fusion.1
  32.1 0.6 slice_subtract_fusion
  32.7 0.0 copy-start.6
  32.7 1.4 %collective-permute-start.4 = (f32[1,32,512]{2,1,0:T(8,128)S(1)}, f32[1,32,512]{2,1,0:T(8,128)S(1)}, u32[]{:S(2)}, u32[]{:S(2)}) collective-permute-start(f32[1,32,512]{2,1,0:T(8,128)S(1)} %slice.127), channel_id=1, source_target_pairs={{8,0},{16,8},{24,16},{9,1},{17,9},{25,17},{10,2},{18,10},{26,18},{... | collective-permute-start | bytes 196616 | tf_op jit(solution)/shard_map/ppermute | solution.py:16
  34.1 0.2 slice_subtract_fusion.4
  34.4 1.3 %collective-permute-start.6 = (f32[32,1,512]{2,1,0:T(1,128)S(1)}, f32[32,1,512]{2,1,0:T(1,128)S(1)}, u32[]{:S(2)}, u32[]{:S(2)}) collective-permute-start(f32[32,1,512]{2,1,0:T(1,128)S(1)} %slice.133), channel_id=1, source_target_pairs={{1,0},{2,1},{3,2},{4,3},{5,4},{6,5},{7,6},{9,8},{10,9},{11,10},{12... | collective-permute-start | bytes 196616 | tf_op jit(solution)/shard_map/ppermute | solution.py:16
  35.7 4.2 %collective-permute-done.4 = f32[1,32,512]{2,1,0:T(8,128)S(1)} collective-permute-done((f32[1,32,512]{2,1,0:T(8,128)S(1)}, f32[1,32,512]{2,1,0:T(8,128)S(1)}, u32[]{:S(2)}, u32[]{:S(2)}) %collective-permute-start.4) | collective-permute-done | bytes 65568 | tf_op jit(solution)/shard_map/ppermute | solution.py:16
  39.9 0.0 collective-permute-done.6
  39.9 0.1 fusion.21
  40.0 0.0 copy-done.6
  40.0 3.8 %multiply_reduce_fusion.6 = (f32[]{:T(128)}, f32[]{:T(128)}, f32[32,32,512]{2,1,0:T(8,128)S(1)}, f32[]{:T(128)}, f32[32,32,512]{2,1,0:T(8,128)}, /*index=5*/f32[...) fusion(f32[32,32,512]{2,1,0:T(8,128)S(1)} %get-tuple-element.23, f32[32,32,512]{2,1,0:T(8,128)S(1)} %copy-done.6, ...), kind=kLoop, calls=%fused_computation.38 | loop fusion | flops 15728634 | bytes 20967448 | tf_op jit(solution)/shard_map/reduce_sum | solution.py:66
  43.8 0.0 copy-start.1
  43.8 0.0 copy-start.4
  43.8 0.1 slice.135
  43.9 2.7 %collective-permute-start.7 = (f32[32,1,512]{2,1,0:T(1,128)S(1)}, f32[32,1,512]{2,1,0:T(1,128)S(1)}, u32[]{:S(2)}, u32[]{:S(2)}) collective-permute-start(f32[32,1,512]{2,1,0:T(1,128)S(1)} %slice.135), channel_id=1, source_target_pairs={{0,1},{1,2},{2,3},{3,4},{4,5},{5,6},{6,7},{8,9},{9,10},{10,11},{11... | collective-permute-start | bytes 196616 | tf_op jit(solution)/shard_map/ppermute | solution.py:16
  46.6 4.7 %collective-permute-start.5 = (f32[1,32,512]{2,1,0:T(8,128)S(1)}, f32[1,32,512]{2,1,0:T(8,128)S(1)}, u32[]{:S(2)}, u32[]{:S(2)}) collective-permute-start(f32[1,32,512]{2,1,0:T(8,128)S(1)} %slice.129), channel_id=1, source_target_pairs={{0,8},{8,16},{16,24},{1,9},{9,17},{17,25},{2,10},{10,18},{18,26},{... | collective-permute-start | bytes 196616 | tf_op jit(solution)/shard_map/ppermute | solution.py:16
  51.4 1.5 %slice.130 = f32[31,32,512]{2,1,0:T(8,128)} slice(f32[32,32,512]{2,1,0:T(8,128)S(1)} %get-tuple-element.14), slice={[0:31], [0:32], [0:512]} | slice | bytes 4063232 | tf_op jit(solution)/shard_map/slice | solution.py:60
  52.9 0.0 copy-done.1
  52.9 0.0 copy-done.4
  56.6 0.0 collective-permute-done.7
  56.7 0.0 collective-permute-done.5
  56.7 0.0 copy-start.2
  56.7 0.0 copy-start.3
  56.7 0.0 copy-start.5
  56.7 8.3 %multiply_reduce_fusion.7 = (f32[]{:T(128)}, f32[]{:T(128)}, f32[32,32,512]{2,1,0:T(8,128)}) fusion(f32[32,32,512]{2,1,0:T(8,128)S(1)} %copy-done, f32[32,32,512]{2,1,0:T(8,128)} %get-tuple-element.16, f32[32,32,512]{2,1,0:T(8,128)} %get-tuple-element.18, f32[32,32,511]{2,1,0:T(8,128)} %bitcast.19, f32[32,32,512]{2,1,0:T(8,128)} %copy-done.1, ...), kind=kLoop, calls=%fused_computation.39 | loop fusion | flops 9961470 | bytes 18870280 | tf_op jit(solution)/shard_map/reduce_sum | solution.py:64
  65.0 1.4 %maximum_bitcast_fusion = (f32[1,2]{1,0:T(1,128)S(1)}, f32[1,2]{1,0:T(1,128)S(1)}) fusion(f32[1]{0:T(128)} %bitcast.4, f32[1]{0:T(128)} %bitcast.3, f32[1]{0:T(128)} %bitcast.7, f32[1]{0:T(128)} %bitcast.6), kind=kLoop, calls=%fused_computation.54 | loop fusion | flops 4 | bytes 32 | tf_op jit(solution)/shard_map/stack | solution.py:30
  66.3 0.0 copy-done.2
  66.3 0.0 copy-done.3
  66.3 0.0 copy-done.5
  66.4 3.4 %pad_maximum_fusion = f32[3,32,32,512]{3,2,1,0:T(8,128)} fusion(f32[1,32,32,512]{3,2,1,0:T(8,128)S(1)} %bitcast.20, f32[1,32,32,512]{3,2,1,0:T(8,128)S(1)} %bitcast.17, f32[1,32,32,512]{3,2,1,0:T(8,128)S(1)} %bitcast.21), kind=kLoop, calls=%fused_computation | loop fusion | flops 3145728 | bytes 12582912 | tf_op jit(solution)/shard_map/stack | solution.py:75
  69.8 40.5 %psum.7 = f32[2,2]{1,0:T(2,128)S(1)} all-reduce(f32[2,2]{1,0:T(2,128)S(1)} %pad_maximum_fusion.1), channel_id=1, replica_groups=mesh['inl'=4,'xln'=8] {'inl','xln'}, use_global_device_ids=true, to_apply=%region_8.9 | all-reduce | flops 4 | bytes 32 | tf_op jit(solution)/shard_map/psum | solution.py:30
  110.2 0.6 sqrt.3
  (7 shorter events, 0.1 us)
Async XLA Ops:
  1.5 11.5 %collective-permute-start = (f32[1,32,512]{2,1,0:T(8,128)S(1)}, f32[1,32,512]{2,1,0:T(8,128)S(1)}, u32[]{:S(2)}, u32[]{:S(2)}) collective-permute-start(f32[1,32,512]{2,1,0:T(8,128)S(1)} %slice.92), channel_id=1, source_target_pairs={{8,0},{16,8},{24,16},{9,1},{17,9},{25,17},{10,2},{18,10},{26,18},{... | collective-permute-start | bytes 196616 | tf_op jit(solution)/shard_map/ppermute | solution.py:16
  3.8 5.5 %copy-start = (f32[32,32,512]{2,1,0:T(8,128)S(1)}, f32[32,32,512]{2,1,0:T(8,128)}, u32[]{:S(2)}) copy-start(f32[32,32,512]{2,1,0:T(8,128)} %param.2) | copy-start | bytes 6291460
  3.9 9.2 %collective-permute-start.2 = (f32[32,1,512]{2,1,0:T(1,128)S(1)}, f32[32,1,512]{2,1,0:T(1,128)S(1)}, u32[]{:S(2)}, u32[]{:S(2)}) collective-permute-start(f32[32,1,512]{2,1,0:T(1,128)S(1)} %slice.98), channel_id=1, source_target_pairs={{1,0},{2,1},{3,2},{4,3},{5,4},{6,5},{7,6},{9,8},{10,9},{11,10},{12... | collective-permute-start | bytes 196616 | tf_op jit(solution)/shard_map/ppermute | solution.py:16
  17.7 8.9 %collective-permute-start.3 = (f32[32,1,512]{2,1,0:T(1,128)S(1)}, f32[32,1,512]{2,1,0:T(1,128)S(1)}, u32[]{:S(2)}, u32[]{:S(2)}) collective-permute-start(f32[32,1,512]{2,1,0:T(1,128)S(1)} %slice.122), channel_id=1, source_target_pairs={{0,1},{1,2},{2,3},{3,4},{4,5},{5,6},{6,7},{8,9},{9,10},{10,11},{11... | collective-permute-start | bytes 196616 | tf_op jit(solution)/shard_map/ppermute | solution.py:16
  20.8 7.5 %collective-permute-start.1 = (f32[1,32,512]{2,1,0:T(8,128)S(1)}, f32[1,32,512]{2,1,0:T(8,128)S(1)}, u32[]{:S(2)}, u32[]{:S(2)}) collective-permute-start(f32[1,32,512]{2,1,0:T(8,128)S(1)} %slice.120), channel_id=1, source_target_pairs={{0,8},{8,16},{16,24},{1,9},{9,17},{17,25},{2,10},{10,18},{18,26},{... | collective-permute-start | bytes 196616 | tf_op jit(solution)/shard_map/ppermute | solution.py:16
  32.7 7.3 %copy-start.6 = (f32[32,32,512]{2,1,0:T(8,128)S(1)}, f32[32,32,512]{2,1,0:T(8,128)}, u32[]{:S(2)}) copy-start(f32[32,32,512]{2,1,0:T(8,128)} %param.3) | copy-start | bytes 6291460
  32.7 7.2 %collective-permute-start.4 = (f32[1,32,512]{2,1,0:T(8,128)S(1)}, f32[1,32,512]{2,1,0:T(8,128)S(1)}, u32[]{:S(2)}, u32[]{:S(2)}) collective-permute-start(f32[1,32,512]{2,1,0:T(8,128)S(1)} %slice.127), channel_id=1, source_target_pairs={{8,0},{16,8},{24,16},{9,1},{17,9},{25,17},{10,2},{18,10},{26,18},{... | collective-permute-start | bytes 196616 | tf_op jit(solution)/shard_map/ppermute | solution.py:16
  34.4 5.5 %collective-permute-start.6 = (f32[32,1,512]{2,1,0:T(1,128)S(1)}, f32[32,1,512]{2,1,0:T(1,128)S(1)}, u32[]{:S(2)}, u32[]{:S(2)}) collective-permute-start(f32[32,1,512]{2,1,0:T(1,128)S(1)} %slice.133), channel_id=1, source_target_pairs={{1,0},{2,1},{3,2},{4,3},{5,4},{6,5},{7,6},{9,8},{10,9},{11,10},{12... | collective-permute-start | bytes 196616 | tf_op jit(solution)/shard_map/ppermute | solution.py:16
  43.8 9.1 %copy-start.1 = (f32[32,32,512]{2,1,0:T(8,128)}, f32[32,32,512]{2,1,0:T(8,128)S(1)}, u32[]{:S(2)}) copy-start(f32[32,32,512]{2,1,0:T(8,128)S(1)} %get-tuple-element.21) | copy-start | bytes 6291460
  43.8 9.1 %copy-start.4 = (f32[32,32,512]{2,1,0:T(8,128)}, f32[32,32,512]{2,1,0:T(8,128)S(1)}, u32[]{:S(2)}) copy-start(f32[32,32,512]{2,1,0:T(8,128)S(1)} %get-tuple-element.14) | copy-start | bytes 6291460
  43.9 12.7 %collective-permute-start.7 = (f32[32,1,512]{2,1,0:T(1,128)S(1)}, f32[32,1,512]{2,1,0:T(1,128)S(1)}, u32[]{:S(2)}, u32[]{:S(2)}) collective-permute-start(f32[32,1,512]{2,1,0:T(1,128)S(1)} %slice.135), channel_id=1, source_target_pairs={{0,1},{1,2},{2,3},{3,4},{4,5},{5,6},{6,7},{8,9},{9,10},{10,11},{11... | collective-permute-start | bytes 196616 | tf_op jit(solution)/shard_map/ppermute | solution.py:16
  46.6 10.0 %collective-permute-start.5 = (f32[1,32,512]{2,1,0:T(8,128)S(1)}, f32[1,32,512]{2,1,0:T(8,128)S(1)}, u32[]{:S(2)}, u32[]{:S(2)}) collective-permute-start(f32[1,32,512]{2,1,0:T(8,128)S(1)} %slice.129), channel_id=1, source_target_pairs={{0,8},{8,16},{16,24},{1,9},{9,17},{17,25},{2,10},{10,18},{18,26},{... | collective-permute-start | bytes 196616 | tf_op jit(solution)/shard_map/ppermute | solution.py:16
  56.7 9.7 %copy-start.2 = (f32[32,32,512]{2,1,0:T(8,128)S(1)}, f32[32,32,512]{2,1,0:T(8,128)}, u32[]{:S(2)}) copy-start(f32[32,32,512]{2,1,0:T(8,128)} %copy-done.1) | copy-start | bytes 6291460
  56.7 9.7 %copy-start.3 = (f32[32,32,512]{2,1,0:T(8,128)S(1)}, f32[32,32,512]{2,1,0:T(8,128)}, u32[]{:S(2)}) copy-start(f32[32,32,512]{2,1,0:T(8,128)} %get-tuple-element.18) | copy-start | bytes 6291460
  56.7 9.7 %copy-start.5 = (f32[32,32,512]{2,1,0:T(8,128)S(1)}, f32[32,32,512]{2,1,0:T(8,128)}, u32[]{:S(2)}) copy-start(f32[32,32,512]{2,1,0:T(8,128)} %copy-done.4) | copy-start | bytes 6291460
where the time goes:
time: 111 us
  blocking collectives  40.5 us (36%)
  other arithmetic  33.9 us (31%)
  starting transfers between devices  21.5 us (19%)
  waiting for transfers between devices  5.79 us (5%)
  between operations  4.65 us (4%)
  local copies, waits for them, and re-layouts  4.5 us (4%)
    psum x1, blocking collectives, finish(): return jnp.sqrt(lax.psum(jnp.stack(sums_list), ('inl', 'xln')))  40.5 us
    ppermute x8, starting transfers between devices, passed_along(): lax.ppermute(value, axis, [(source, source + steps) for source in range(f...  21.5 us
    reduce_sum x1, other arithmetic, per_device(): primal_sum = jnp.sum((updated - primal) ** 2)  8.26 us
    ppermute x8, waiting for transfers between devices, passed_along(): lax.ppermute(value, axis, [(source, source + steps) for source in range(f...  5.79 us
    min x1, other arithmetic, per_device(): fresh_i = jnp.clip(dual_i + SIGMA * grad_i, -bound, bound)  4.53 us
    sub x2, other arithmetic, per_device(): smooth[:, 1:] - smooth[:, :-1]  4.4 us
    reduce_sum x1, other arithmetic, per_device(): jnp.sum((fresh_i - dual_i) ** 2) + jnp.sum((fresh_x - dual_x) ** 2)  3.83 us
    sub x1, other arithmetic, per_device(): smooth = 2.0 * updated - primal  3.47 us
  transfers between devices with their start and end apart: 8, of which 2 were waited for; matrix products, arithmetic and copies ran while one was open for 10% of the time, Pallas kernels for 0%

commit v1 on v0

v1 whole, which is shorter than its diff:
```python
import functools

import jax
import jax.numpy as jnp
from jax import lax
from jax.experimental import pallas as pl
from jax.experimental.pallas import tpu as pltpu
from jax.sharding import PartitionSpec as P

SIGMA = 0.28
TAU = 0.28
GAIN = TAU / (1.0 + TAU)


def clip(value, limit):
    return jnp.minimum(jnp.maximum(value, -limit), limit)


def fold(square):
    rows, lanes = square.shape
    total = square[0:8]
    for at in range(8, rows, 8):
        total = total + square[at : at + 8]
    part = total[:, 0:128]
    for at in range(128, lanes, 128):
        part = part + total[:, at : at + 128]
    return part


def kernel(
    ni_dev, nx_dev,
    noisy, bound, out, dual, norms,
    n, b, v, step,
    nx_first, nx_last, bx_last, nx_next, nx_prev, bx_prev,
    vx_first, vx_last, vx_next, vx_prev, dx_prev, di_prev,
    mine, others_x, others_i,
    load_sem, send_sem, recv_sem, xs_sem, xr_sem, is_sem, ir_sem,
):
    ni, nx, nz = noisy.shape
    top, end = ni, ni + 1
    my_i, my_x = lax.axis_index("inl"), lax.axis_index("xln")

    loads = []

    def load(src, dst):
        copy = pltpu.make_async_copy(src, dst, load_sem.at[len(loads)])
        copy.start()
        loads.append(copy)

    load(noisy.at[pl.ds(ni - 1, 1)], n.at[pl.ds(top, 1)])
    load(bound.at[pl.ds(ni - 1, 1)], b.at[pl.ds(top, 1)])
    load(noisy.at[pl.ds(0, 1)], n.at[pl.ds(1, 1)])
    load(noisy.at[pl.ds(1, ni - 2)], n.at[pl.ds(2, ni - 2)])
    load(bound.at[pl.ds(0, ni - 1)], b.at[pl.ds(1, ni - 1)])

    barrier = pltpu.get_barrier_semaphore()
    for axis, me, count in (("inl", my_i, ni_dev), ("xln", my_x, nx_dev)):
        for k in range(1, count):
            pl.semaphore_signal(
                barrier, inc=1, device_id={axis: lax.rem(me + k, count)},
                device_id_type=pl.DeviceIdType.MESH,
            )
    pl.semaphore_wait(barrier, ni_dev + nx_dev - 2)

    sent = []

    def send(slot, src, dst, axis, forward):
        me, count = (my_i, ni_dev) if axis == "inl" else (my_x, nx_dev)
        target = lax.rem(me + (1 if forward else count - 1), count)
        copy = pltpu.make_async_remote_copy(
            src_ref=src, dst_ref=dst, send_sem=send_sem.at[slot], recv_sem=recv_sem.at[slot],
            device_id={axis: target}, device_id_type=pl.DeviceIdType.MESH,
        )
        not_last, not_first = me < count - 1, me > 0
        can_send, can_recv = (not_last, not_first) if forward else (not_first, not_last)

        @pl.when(can_send)
        def _():
            copy.start()

        sent.append((copy, can_send))

        def arrive(fill):
            @pl.when(can_recv)
            def _():
                copy.wait_recv()

            @pl.when(jnp.logical_not(can_recv))
            def _():
                fill()

        return arrive

    def setter(dst, src):
        def fill():
            dst[...] = src[...]

        return fill

    loads[0].wait()
    got_n_prev = send(0, n.at[top], n.at[0], "inl", True)
    loads[1].wait()
    got_b_prev = send(1, b.at[top], b.at[0], "inl", True)
    loads[2].wait()
    got_n_next = send(2, n.at[1], n.at[end], "inl", False)
    loads[3].wait()
    nx_last[...] = n[1:end, nx - 1, :]
    got_nx_prev = send(3, nx_last, nx_prev, "xln", True)
    nx_first[...] = n[1:end, 0, :]
    got_nx_next = send(5, nx_first, nx_next, "xln", False)
    loads[4].wait()
    bx_last[...] = b[1:end, nx - 1, :]
    got_bx_prev = send(4, bx_last, bx_prev, "xln", True)

    row = lax.broadcasted_iota(jnp.int32, (nx, nz), 0)
    lane = lax.broadcasted_iota(jnp.int32, (nx, nz), 1)
    first_row, last_row = row == 0, row == nx - 1
    first_lane, last_lane = lane == 0, lane == nz - 1

    step[...] = jnp.zeros_like(step)

    def pass_one(i, carry):
        here, limit = n[i + 1], b[i + 1]
        di = clip(SIGMA * (n[i + 2] - here), limit)
        dx = clip(SIGMA * jnp.where(last_row, 0.0, pltpu.roll(here, nx - 1, 0) - here), limit)
        dz = clip(SIGMA * jnp.where(last_lane, 0.0, pltpu.roll(here, nz - 1, 1) - here), limit)
        dual[0, i] = di
        dual[1, i] = dx
        dual[2, i] = dz
        div = di - step[...]
        div = div + (dx - jnp.where(first_row, 0.0, pltpu.roll(dx, 1, 0)))
        div = div + (dz - jnp.where(first_lane, 0.0, pltpu.roll(dz, 1, 1)))
        step[...] = di
        v[i + 1] = here + (2.0 * GAIN) * div
        return carry

    lax.fori_loop(0, ni - 1, pass_one, 0)
    here, limit = n[top], b[top]
    dx = clip(SIGMA * jnp.where(last_row, 0.0, pltpu.roll(here, nx - 1, 0) - here), limit)
    dz = clip(SIGMA * jnp.where(last_lane, 0.0, pltpu.roll(here, nz - 1, 1) - here), limit)
    dual[1, ni - 1] = dx
    dual[2, ni - 1] = dz
    div = (dx - jnp.where(first_row, 0.0, pltpu.roll(dx, 1, 0))) - step[...]
    div = div + (dz - jnp.where(first_lane, 0.0, pltpu.roll(dz, 1, 1)))
    v[top] = here + (2.0 * GAIN) * div

    got_nx_prev(setter(nx_prev, nx_first))
    got_bx_prev(setter(bx_prev, bx_last))
    got_nx_next(setter(nx_next, nx_last))
    dx_last = clip(SIGMA * (nx_next[...] - nx_last[...]), bx_last[...])
    dxp = clip(SIGMA * (nx_first[...] - nx_prev[...]), bx_prev[...])
    dual[1, :, nx - 1, :] = dx_last
    dx_prev[...] = dxp
    v[1:end, nx - 1, :] = v[1:end, nx - 1, :] + (2.0 * GAIN) * dx_last
    v[1:end, 0, :] = v[1:end, 0, :] - (2.0 * GAIN) * dxp

    got_n_prev(setter(n.at[0], n.at[1]))
    got_b_prev(setter(b.at[0], b.at[1]))
    got_n_next(setter(n.at[end], n.at[top]))
    di_last = clip(SIGMA * (n[end] - n[top]), b[top])
    dip = clip(SIGMA * (n[1] - n[0]), b[0])
    dual[0, ni - 1] = di_last
    di_prev[...] = dip
    v[top] = v[top] + (2.0 * GAIN) * di_last
    v[1] = v[1] - (2.0 * GAIN) * dip

    got_v_prev = send(6, v.at[top], v.at[0], "inl", True)
    got_v_next = send(7, v.at[1], v.at[end], "inl", False)
    vx_last[...] = v[1:end, nx - 1, :]
    got_vx_prev = send(8, vx_last, vx_prev, "xln", True)
    vx_first[...] = v[1:end, 0, :]
    got_vx_next = send(9, vx_first, vx_next, "xln", False)

    got_vx_prev(setter(vx_prev, vx_first))
    got_vx_next(setter(vx_next, vx_last))
    got_v_prev(setter(v.at[0], v.at[1]))
    got_v_next(setter(v.at[end], v.at[top]))
    dx_prev[...] = clip(dx_prev[...] + SIGMA * (vx_first[...] - vx_prev[...]), bx_prev[...])
    step[...] = clip(di_prev[...] + SIGMA * (v[1] - v[0]), b[0])

    def pass_two(i, sums):
        p1, d1, p2, d2 = sums
        here, limit, base = v[i + 1], b[i + 1], n[i + 1]
        oi, ox, oz = dual[0, i], dual[1, i], dual[2, i]
        di = clip(oi + SIGMA * (v[i + 2] - here), limit)
        ahead = jnp.where(last_row, vx_next[pl.ds(i, 1), :], pltpu.roll(here, nx - 1, 0))
        dx = clip(ox + SIGMA * (ahead - here), limit)
        dz = clip(
            oz + SIGMA * jnp.where(last_lane, 0.0, pltpu.roll(here, nz - 1, 1) - here), limit
        )
        dual[0, i] = di
        dual[1, i] = dx
        dual[2, i] = dz
        div = di - step[...]
        div = div + (dx - jnp.where(first_row, dx_prev[pl.ds(i, 1), :], pltpu.roll(dx, 1, 0)))
        div = div + (dz - jnp.where(first_lane, 0.0, pltpu.roll(dz, 1, 1)))
        step[...] = di
        half = 0.5 * (here - base)
        change = GAIN * (div - half)
        out[i] = base + half + change
        p1 = p1 + fold(half * half)
        d1 = d1 + fold(oi * oi + ox * ox + oz * oz)
        p2 = p2 + fold(change * change)
        oi, ox, oz = di - oi, dx - ox, dz - oz
        d2 = d2 + fold(oi * oi + ox * ox + oz * oz)
        return p1, d1, p2, d2

    zero = jnp.zeros((8, 128), jnp.float32)
    sums = lax.fori_loop(0, ni, pass_two, (zero,) * 4)

    for k in range(4):
        mine[0, k] = sums[k]

    def reduce(count, me, axis, source, others, ss, rs):
        copies = []
        for k in range(1, count):
            copy = pltpu.make_async_remote_copy(
                src_ref=source, dst_ref=others.at[k - 1],
                send_sem=ss.at[k - 1], recv_sem=rs.at[k - 1],
                device_id={axis: lax.rem(me + k, count)}, device_id_type=pl.DeviceIdType.MESH,
            )
            copy.start()
            copies.append(copy)
        total = source[...]
        for copy in copies:
            copy.wait_recv()
        for k in range(count - 1):
            total = total + others[k]
        return total, copies

    total, copies_x = reduce(nx_dev, my_x, "xln", mine.at[0], others_x, xs_sem, xr_sem)
    mine[1] = total
    total, copies_i = reduce(ni_dev, my_i, "inl", mine.at[1], others_i, is_sem, ir_sem)
    at = 2 * lax.broadcasted_iota(jnp.int32, (2, 2), 0) + lax.broadcasted_iota(jnp.int32, (2, 2), 1)
    result = jnp.zeros((2, 2), jnp.float32)
    for k in range(4):
        result = jnp.where(at == k, jnp.sum(total[k]), result)
    norms[...] = jnp.sqrt(result)

    for copy in copies_x + copies_i:
        copy.wait_send()
    for copy, can_send in sent:
        @pl.when(can_send)
        def _():
            copy.wait_send()


def per_device(noisy, bound):
    ni, nx, nz = noisy.shape
    ni_dev, nx_dev = lax.axis_size("inl"), lax.axis_size("xln")
    f32 = jnp.float32
    face = pltpu.VMEM((ni, nz), f32)
    slab = pltpu.VMEM((nx, nz), f32)
    dma = pltpu.SemaphoreType.DMA
    volume = 4 * ni * nx * nz
    return pl.pallas_call(
        functools.partial(kernel, ni_dev, nx_dev),
        out_shape=(
            pltpu.VMEM((ni, nx, nz), f32),
            pltpu.VMEM((3, ni, nx, nz), f32),
            jax.ShapeDtypeStruct((2, 2), f32),
        ),
        in_specs=[pl.BlockSpec(memory_space=pltpu.HBM)] * 2,
        out_specs=(
            pl.BlockSpec(memory_space=pltpu.VMEM),
            pl.BlockSpec(memory_space=pltpu.VMEM),
            pl.BlockSpec(memory_space=pltpu.VMEM),
        ),
        scratch_shapes=[
            pltpu.VMEM((ni + 2, nx, nz), f32),
            pltpu.VMEM((ni + 1, nx, nz), f32),
            pltpu.VMEM((ni + 2, nx, nz), f32),
            slab,
            *([face] * 11),
            slab,
            pltpu.VMEM((2, 4, 8, 128), f32),
            pltpu.VMEM((nx_dev - 1, 4, 8, 128), f32),
            pltpu.VMEM((ni_dev - 1, 4, 8, 128), f32),
            dma((5,)), dma((10,)), dma((10,)),
            dma((nx_dev - 1,)), dma((nx_dev - 1,)), dma((ni_dev - 1,)), dma((ni_dev - 1,)),
        ],
        compiler_params=pltpu.CompilerParams(
            collective_id=0, has_side_effects=True, vmem_limit_bytes=24 * 1024 * 1024
        ),
        cost_estimate=pl.CostEstimate(
            flops=80 * ni * nx * nz, bytes_accessed=6 * volume, transcendentals=0
        ),
        name="denoise",
    )(noisy, bound)


def solution(mesh):
    in_specs = (P("inl", "xln", None), P("inl", "xln", None))
    out_specs = (P("inl", "xln", None), P(None, "inl", "xln", None), P())
    return jax.shard_map(
        per_device, mesh=mesh, in_specs=in_specs, out_specs=out_specs, check_vma=False
    )
```

time: 111 us -> 37.2 us (0.34)
  blocking collectives: 40.5 us -> 0 us
  other arithmetic: 33.9 us -> 0 us
  Pallas kernels: 0 us -> 28.6 us
  starting transfers between devices: 21.5 us -> 0 us
  waiting for transfers between devices: 5.79 us -> 0 us
  between operations: 4.65 us -> 0.65 us
  local copies, waits for them, and re-layouts: 4.5 us -> 7.76 us
    psum x1 -> x0, blocking collectives: 40.5 us -> none  [finish(): return jnp.sqrt(lax.psum(jnp.stack(sums_list), ('inl', 'xln')))]
    pallas_call x0 -> x1, Pallas kernels: none -> 28.6 us  [per_device(): pl.pallas_call(functools.partial(kernel, ni_dev, nx_dev), out_shape=(pltp...]
    ppermute x8 -> x0, starting transfers between devices: 21.5 us -> none  [passed_along(): lax.ppermute(value, axis, [(source, source + steps) for source in range(f...]
    sub x7 -> x0, other arithmetic: 12.3 us -> none  [the longest x2 4.4 us: per_device(): smooth[:, 1:] - smooth[:, :-1]]
    reduce_sum x2 -> x0, other arithmetic: 12.1 us -> none  [the longest x1 8.26 us: per_device(): primal_sum = jnp.sum((updated - primal) ** 2)]
    unnamed x14 -> x7, local copies, waits for them, and re-layouts: 0.03 us -> 7.76 us
    ppermute x8 -> x0, waiting for transfers between devices: 5.79 us -> none  [passed_along(): lax.ppermute(value, axis, [(source, source + steps) for source in range(f...]
    another operation x3 -> x0, other arithmetic: 4.77 us -> none  [the longest x1 3.41 us: per_device(): return (primal, jnp.stack([dual_i, dual_x, dual_z]), norms)]
  transfers between devices with their start and end apart: 8 -> 0, of which waited for: 2 -> 0; matrix products, arithmetic and copies ran while one was open for 10% -> 0% of each run, Pallas kernels for 0% -> 0%
where the time goes in v1:
time: 37.2 us; the launch traced here: 37.1 us
  Pallas kernels  28.6 us (77%)
  local copies, waits for them, and re-layouts  7.76 us (21%)
  between operations  0.65 us (2%)
    pallas_call x1, Pallas kernels, per_device(): pl.pallas_call(functools.partial(kernel, ni_dev, nx_dev), out_shape=(pltp...  28.6 us
    unnamed x7, local copies, waits for them, and re-layouts  7.76 us

profile of v1, /device:TPU:0, one launch (start us, length us, event | category | flops | bytes accessed | tf_op | source)
XLA Modules:
  0.0 37.1 jit_solution(12833960618633498811)
XLA Ops:
  0.6 0.0 copy-start
  0.6 1.6 %copy-done = f32[32,32,512]{2,1,0:T(8,128)S(1)} copy-done((f32[32,32,512]{2,1,0:T(8,128)S(1)}, f32[32,32,512]{2,1,0:T(8,128)}, u32[]{:S(2)}) %copy-start) | copy-done | bytes 2097176
  2.2 0.0 copy-start.1
  2.2 1.6 %copy-done.1 = f32[32,32,512]{2,1,0:T(8,128)S(1)} copy-done((f32[32,32,512]{2,1,0:T(8,128)S(1)}, f32[32,32,512]{2,1,0:T(8,128)}, u32[]{:S(2)}) %copy-start.1) | copy-done | bytes 2097176
  3.8 28.6 %denoise.1 = (f32[32,32,512]{2,1,0:T(8,128)S(1)}, f32[3,32,32,512]{3,2,1,0:T(8,128)S(1)}, f32[2,2]{1,0:T(2,128)S(1)}) custom-call(f32[32,32,512]{2,1,0:T(8,128)S(1)} %copy-done, f32[32,32,512]{2,1,0:T(8,128)S(1)} %copy-done.1), custom_call_target="tpu_custom_call" | custom-call | flops 41943040 | bytes 12582912 | tf_op jit(solution)/shard_map/denoise/pallas_call | solution.py:256
  32.5 1.3 %copy.8 = f32[32,32,512]{2,1,0:T(8,128)} copy(f32[32,32,512]{2,1,0:T(8,128)S(1)} %get-tuple-element.3) | data formatting | bytes 4194304
  33.8 2.7 %copy.9 = f32[3,32,32,512]{3,2,1,0:T(8,128)} copy(f32[3,32,32,512]{3,2,1,0:T(8,128)S(1)} %get-tuple-element.4) | data formatting | bytes 12582912
  36.5 0.6 %copy.10 = f32[2,2]{1,0:T(2,128)} copy(f32[2,2]{1,0:T(2,128)S(1)} %get-tuple-element.11) | data formatting | bytes 32
Async XLA Ops:
  0.6 1.6 %copy-start = (f32[32,32,512]{2,1,0:T(8,128)S(1)}, f32[32,32,512]{2,1,0:T(8,128)}, u32[]{:S(2)}) copy-start(f32[32,32,512]{2,1,0:T(8,128)} %noisy.1) | copy-start | bytes 6291460
  2.2 1.6 %copy-start.1 = (f32[32,32,512]{2,1,0:T(8,128)S(1)}, f32[32,32,512]{2,1,0:T(8,128)}, u32[]{:S(2)}) copy-start(f32[32,32,512]{2,1,0:T(8,128)} %bound.1) | copy-start | bytes 6291460

commit v2 on v1

--- a/solution.py
+++ b/solution.py
@@ -245,6 +245,21 @@
             copy.wait_send()
 
 
+def put_out(out_held, dual_held, norms_held, out, dual, norms, sems):
+    half = out.shape[0] // 2
+    pairs = [(norms_held, norms)]
+    for at in (0, half):
+        part = pl.ds(at, half)
+        pairs.append((out_held.at[part], out.at[part]))
+        for axis in range(3):
+            pairs.append((dual_held.at[axis, part], dual.at[axis, part]))
+    copies = [pltpu.make_async_copy(src, dst, sems.at[k]) for k, (src, dst) in enumerate(pairs)]
+    for copy in copies:
+        copy.start()
+    for copy in copies:
+        copy.wait()
+
+
 def per_device(noisy, bound):
     ni, nx, nz = noisy.shape
     ni_dev, nx_dev = lax.axis_size("inl"), lax.axis_size("xln")
@@ -253,12 +268,14 @@
     slab = pltpu.VMEM((nx, nz), f32)
     dma = pltpu.SemaphoreType.DMA
     volume = 4 * ni * nx * nz
-    return pl.pallas_call(
+    noisy = pltpu.with_memory_space_constraint(noisy, pltpu.HBM)
+    bound = pltpu.with_memory_space_constraint(bound, pltpu.HBM)
+    held = pl.pallas_call(
         functools.partial(kernel, ni_dev, nx_dev),
         out_shape=(
             pltpu.VMEM((ni, nx, nz), f32),
             pltpu.VMEM((3, ni, nx, nz), f32),
-            jax.ShapeDtypeStruct((2, 2), f32),
+            pltpu.VMEM((2, 2), f32),
         ),
         in_specs=[pl.BlockSpec(memory_space=pltpu.HBM)] * 2,
         out_specs=(
@@ -287,6 +304,22 @@
         ),
         name="denoise",
     )(noisy, bound)
+    in_vmem = pl.BlockSpec(memory_space=pltpu.VMEM)
+    in_hbm = pl.BlockSpec(memory_space=pltpu.HBM)
+    return pl.pallas_call(
+        put_out,
+        out_shape=(
+            jax.ShapeDtypeStruct((ni, nx, nz), f32),
+            jax.ShapeDtypeStruct((3, ni, nx, nz), f32),
+            jax.ShapeDtypeStruct((2, 2), f32),
+        ),
+        in_specs=[in_vmem] * 3,
+        out_specs=(in_hbm,) * 3,
+        scratch_shapes=[dma((9,))],
+        compiler_params=pltpu.CompilerParams(vmem_limit_bytes=1024 * 1024),
+        cost_estimate=pl.CostEstimate(flops=0, bytes_accessed=4 * volume, transcendentals=0),
+        name="put_out",
+    )(*held)
 
 
 def solution(mesh):

time: 37.2 us -> 32.8 us (0.88)
  local copies, waits for them, and re-layouts: 7.76 us -> 0 us
  Pallas kernels: 28.6 us -> 32 us
    unnamed x7 -> x0, local copies, waits for them, and re-layouts: 7.76 us -> none
    pallas_call x0 -> x1, Pallas kernels: none -> 3.38 us  [per_device(): pl.pallas_call(put_out, out_shape=(jax.ShapeDtypeStruct((ni, nx, nz), f32...]
where the time goes in v2:
time: 32.8 us; the launch traced here: 32.6 us
  Pallas kernels  32 us (98%)
  between operations  0.64 us (2%)
    pallas_call x1, Pallas kernels, per_device(): pl.pallas_call(functools.partial(kernel, ni_dev, nx_dev), out_shape=(pltp...  28.6 us
    pallas_call x1, Pallas kernels, per_device(): pl.pallas_call(put_out, out_shape=(jax.ShapeDtypeStruct((ni, nx, nz), f32...  3.38 us

profile of v2, /device:TPU:0, one launch (start us, length us, event | category | flops | bytes accessed | tf_op | source)
XLA Modules:
  0.0 32.6 jit_solution(8172396366111903228)
XLA Ops:
  0.6 28.6 %denoise.1 = (f32[32,32,512]{2,1,0:T(8,128)S(1)}, f32[3,32,32,512]{3,2,1,0:T(8,128)S(1)}, f32[2,2]{1,0:T(2,128)S(1)}) custom-call(f32[32,32,512]{2,1,0:T(8,128)} %noisy.1, f32[32,32,512]{2,1,0:T(8,128)} %bound.1), custom_call_target="tpu_custom_call" | custom-call | flops 41943040 | bytes 12582912 | tf_op jit(solution)/shard_map/denoise/pallas_call | solution.py:273
  29.3 3.4 %put_out.1 = (f32[32,32,512]{2,1,0:T(8,128)}, f32[3,32,32,512]{3,2,1,0:T(8,128)}, f32[2,2]{1,0:T(2,128)}) custom-call(f32[32,32,512]{2,1,0:T(8,128)S(1)} %get-tuple-element.6.out_held, f32[3,32,32,512]{3,2,1,0:T(8,128)S(1)} %get-tuple-element.7.dual_held, f32[2,2]{1,0:T(2,128)S(1)} %get-tuple-element.8.norms_held), custom_call_target="tpu_custom_call" | custom-call | bytes 8388608 | tf_op jit(solution)/shard_map/put_out/pallas_call | solution.py:309

commit v3 on v2

--- a/solution.py
+++ b/solution.py
@@ -32,7 +32,7 @@
     noisy, bound, out, dual, norms,
     n, b, v, step,
     nx_first, nx_last, bx_last, nx_next, nx_prev, bx_prev,
-    vx_first, vx_last, vx_next, vx_prev, dx_prev, di_prev,
+    vx_first, vx_last, vx_next, vx_prev, dx_prev, dx_edge, di_prev,
     mine, others_x, others_i,
     load_sem, send_sem, recv_sem, xs_sem, xr_sem, is_sem, ir_sem,
 ):
@@ -119,7 +119,10 @@
 
     step[...] = jnp.zeros_like(step)
 
-    def pass_one(i, carry):
+    def squares(oi, ox, oz):
+        return fold(oi * oi + ox * ox + oz * oz)
+
+    def pass_one(i, d1):
         here, limit = n[i + 1], b[i + 1]
         di = clip(SIGMA * (n[i + 2] - here), limit)
         dx = clip(SIGMA * jnp.where(last_row, 0.0, pltpu.roll(here, nx - 1, 0) - here), limit)
@@ -132,9 +135,10 @@
         div = div + (dz - jnp.where(first_lane, 0.0, pltpu.roll(dz, 1, 1)))
         step[...] = di
         v[i + 1] = here + (2.0 * GAIN) * div
-        return carry
-
-    lax.fori_loop(0, ni - 1, pass_one, 0)
+        return d1 + squares(di, dx, dz)
+
+    zero = jnp.zeros((8, 128), jnp.float32)
+    d1 = lax.fori_loop(0, ni - 1, pass_one, zero)
     here, limit = n[top], b[top]
     dx = clip(SIGMA * jnp.where(last_row, 0.0, pltpu.roll(here, nx - 1, 0) - here), limit)
     dz = clip(SIGMA * jnp.where(last_lane, 0.0, pltpu.roll(here, nz - 1, 1) - here), limit)
@@ -143,6 +147,7 @@
     div = (dx - jnp.where(first_row, 0.0, pltpu.roll(dx, 1, 0))) - step[...]
     div = div + (dz - jnp.where(first_lane, 0.0, pltpu.roll(dz, 1, 1)))
     v[top] = here + (2.0 * GAIN) * div
+    d1 = d1 + fold(dx * dx + dz * dz)
 
     got_nx_prev(setter(nx_prev, nx_first))
     got_bx_prev(setter(bx_prev, bx_last))
@@ -151,6 +156,7 @@
     dxp = clip(SIGMA * (nx_first[...] - nx_prev[...]), bx_prev[...])
     dual[1, :, nx - 1, :] = dx_last
     dx_prev[...] = dxp
+    dx_edge[...] = dx_last
     v[1:end, nx - 1, :] = v[1:end, nx - 1, :] + (2.0 * GAIN) * dx_last
     v[1:end, 0, :] = v[1:end, 0, :] - (2.0 * GAIN) * dxp
 
@@ -163,53 +169,70 @@
     di_prev[...] = dip
     v[top] = v[top] + (2.0 * GAIN) * di_last
     v[1] = v[1] - (2.0 * GAIN) * dip
-
     got_v_prev = send(6, v.at[top], v.at[0], "inl", True)
     got_v_next = send(7, v.at[1], v.at[end], "inl", False)
     vx_last[...] = v[1:end, nx - 1, :]
     got_vx_prev = send(8, vx_last, vx_prev, "xln", True)
     vx_first[...] = v[1:end, 0, :]
     got_vx_next = send(9, vx_first, vx_next, "xln", False)
-
-    got_vx_prev(setter(vx_prev, vx_first))
-    got_vx_next(setter(vx_next, vx_last))
-    got_v_prev(setter(v.at[0], v.at[1]))
-    got_v_next(setter(v.at[end], v.at[top]))
-    dx_prev[...] = clip(dx_prev[...] + SIGMA * (vx_first[...] - vx_prev[...]), bx_prev[...])
-    step[...] = clip(di_prev[...] + SIGMA * (v[1] - v[0]), b[0])
+    d1 = d1 + fold(di_last * di_last) + fold(dx_last * dx_last)
+
+    face_row = first_row | last_row
 
     def pass_two(i, sums):
-        p1, d1, p2, d2 = sums
+        p1, p2, d2 = sums
         here, limit, base = v[i + 1], b[i + 1], n[i + 1]
         oi, ox, oz = dual[0, i], dual[1, i], dual[2, i]
         di = clip(oi + SIGMA * (v[i + 2] - here), limit)
-        ahead = jnp.where(last_row, vx_next[pl.ds(i, 1), :], pltpu.roll(here, nx - 1, 0))
-        dx = clip(ox + SIGMA * (ahead - here), limit)
-        dz = clip(
-            oz + SIGMA * jnp.where(last_lane, 0.0, pltpu.roll(here, nz - 1, 1) - here), limit
-        )
+        ahead = jnp.where(last_row, 0.0, pltpu.roll(here, nx - 1, 0) - here)
+        dx = clip(ox + SIGMA * ahead, limit)
+        ahead = jnp.where(last_lane, 0.0, pltpu.roll(here, nz - 1, 1) - here)
+        dz = clip(oz + SIGMA * ahead, limit)
         dual[0, i] = di
         dual[1, i] = dx
         dual[2, i] = dz
         div = di - step[...]
-        div = div + (dx - jnp.where(first_row, dx_prev[pl.ds(i, 1), :], pltpu.roll(dx, 1, 0)))
+        div = div + (dx - jnp.where(first_row, 0.0, pltpu.roll(dx, 1, 0)))
         div = div + (dz - jnp.where(first_lane, 0.0, pltpu.roll(dz, 1, 1)))
         step[...] = di
         half = 0.5 * (here - base)
         change = GAIN * (div - half)
         out[i] = base + half + change
-        p1 = p1 + fold(half * half)
-        d1 = d1 + fold(oi * oi + ox * ox + oz * oz)
-        p2 = p2 + fold(change * change)
-        oi, ox, oz = di - oi, dx - ox, dz - oz
-        d2 = d2 + fold(oi * oi + ox * ox + oz * oz)
-        return p1, d1, p2, d2
-
-    zero = jnp.zeros((8, 128), jnp.float32)
-    sums = lax.fori_loop(0, ni, pass_two, (zero,) * 4)
-
-    for k in range(4):
-        mine[0, k] = sums[k]
+        inner = jnp.where(face_row, 0.0, change)
+        return (
+            p1 + fold(half * half),
+            p2 + fold(inner * inner),
+            d2 + squares(di - oi, dx - ox, dz - oz),
+        )
+
+    step[...] = clip(dual[0, 0] + SIGMA * (v[2] - v[1]), b[1])
+    sums = lax.fori_loop(1, ni - 1, pass_two, (zero,) * 3)
+
+    got_v_next(setter(v.at[end], v.at[top]))
+    sums = pass_two(ni - 1, sums)
+    got_v_prev(setter(v.at[0], v.at[1]))
+    step[...] = clip(di_prev[...] + SIGMA * (v[1] - v[0]), b[0])
+    p1, p2, d2 = pass_two(0, sums)
+
+    got_vx_prev(setter(vx_prev, vx_first))
+    got_vx_next(setter(vx_next, vx_last))
+    was = dx_edge[...]
+    dx_last = clip(was + SIGMA * (vx_next[...] - vx_last[...]), bx_last[...])
+    dual[1, :, nx - 1, :] = dx_last
+    moved = dx_last - was
+    d2 = d2 + fold(moved * moved)
+    u_last = out[:, nx - 1, :] + GAIN * moved
+    out[:, nx - 1, :] = u_last
+    dxp = clip(dx_prev[...] + SIGMA * (vx_first[...] - vx_prev[...]), bx_prev[...])
+    u_first = out[:, 0, :] - GAIN * dxp
+    out[:, 0, :] = u_first
+    change = u_last - (nx_last[...] + 0.5 * (vx_last[...] - nx_last[...]))
+    p2 = p2 + fold(change * change)
+    change = u_first - (nx_first[...] + 0.5 * (vx_first[...] - nx_first[...]))
+    p2 = p2 + fold(change * change)
+
+    for k, part in enumerate((p1, d1, p2, d2)):
+        mine[0, k : k + 1] = jnp.sum(part, axis=0, keepdims=True)
 
     def reduce(count, me, axis, source, others, ss, rs):
         copies = []
@@ -234,7 +257,7 @@
     at = 2 * lax.broadcasted_iota(jnp.int32, (2, 2), 0) + lax.broadcasted_iota(jnp.int32, (2, 2), 1)
     result = jnp.zeros((2, 2), jnp.float32)
     for k in range(4):
-        result = jnp.where(at == k, jnp.sum(total[k]), result)
+        result = jnp.where(at == k, jnp.sum(total[k : k + 1], keepdims=True), result)
     norms[...] = jnp.sqrt(result)
 
     for copy in copies_x + copies_i:
@@ -288,11 +311,11 @@
             pltpu.VMEM((ni + 1, nx, nz), f32),
             pltpu.VMEM((ni + 2, nx, nz), f32),
             slab,
-            *([face] * 11),
+            *([face] * 12),
             slab,
-            pltpu.VMEM((2, 4, 8, 128), f32),
-            pltpu.VMEM((nx_dev - 1, 4, 8, 128), f32),
-            pltpu.VMEM((ni_dev - 1, 4, 8, 128), f32),
+            pltpu.VMEM((2, 4, 128), f32),
+            pltpu.VMEM((nx_dev - 1, 4, 128), f32),
+            pltpu.VMEM((ni_dev - 1, 4, 128), f32),
             dma((5,)), dma((10,)), dma((10,)),
             dma((nx_dev - 1,)), dma((nx_dev - 1,)), dma((ni_dev - 1,)), dma((ni_dev - 1,)),
         ],

time: 32.8 us -> 29.6 us (0.902)
  Pallas kernels: 32 us -> 28.9 us
    pallas_call x1, Pallas kernels: 28.6 us -> 25.5 us  [per_device(): pl.pallas_call(functools.partial(kernel, ni_dev, nx_dev), out_shape=(pltp...]
where the time goes in v3:
time: 29.6 us; the launch traced here: 29.5 us
  Pallas kernels  28.9 us (98%)
  between operations  0.64 us (2%)
    pallas_call x1, Pallas kernels, per_device(): pl.pallas_call(functools.partial(kernel, ni_dev, nx_dev), out_shape=(pltp...  25.5 us
    pallas_call x1, Pallas kernels, per_device(): pl.pallas_call(put_out, out_shape=(jax.ShapeDtypeStruct((ni, nx, nz), f32...  3.38 us

profile of v3, /device:TPU:0, one launch (start us, length us, event | category | flops | bytes accessed | tf_op | source)
XLA Modules:
  0.0 29.5 jit_solution(3045635719622110365)
XLA Ops:
  0.6 25.5 %denoise.1 = (f32[32,32,512]{2,1,0:T(8,128)S(1)}, f32[3,32,32,512]{3,2,1,0:T(8,128)S(1)}, f32[2,2]{1,0:T(2,128)S(1)}) custom-call(f32[32,32,512]{2,1,0:T(8,128)} %noisy.1, f32[32,32,512]{2,1,0:T(8,128)} %bound.1), custom_call_target="tpu_custom_call" | custom-call | flops 41943040 | bytes 12582912 | tf_op jit(solution)/shard_map/denoise/pallas_call | solution.py:296
  26.1 3.4 %put_out.1 = (f32[32,32,512]{2,1,0:T(8,128)}, f32[3,32,32,512]{3,2,1,0:T(8,128)}, f32[2,2]{1,0:T(2,128)}) custom-call(f32[32,32,512]{2,1,0:T(8,128)S(1)} %get-tuple-element.6.out_held, f32[3,32,32,512]{3,2,1,0:T(8,128)S(1)} %get-tuple-element.7.dual_held, f32[2,2]{1,0:T(2,128)S(1)} %get-tuple-element.8.norms_held), custom_call_target="tpu_custom_call" | custom-call | bytes 8388608 | tf_op jit(solution)/shard_map/put_out/pallas_call | solution.py:332

commit v4 on v3

--- a/solution.py
+++ b/solution.py
@@ -25,6 +25,31 @@
     for at in range(128, lanes, 128):
         part = part + total[:, at : at + 128]
     return part
+
+
+def greeted(axis, count):
+    return [k for k in range(1, count) if axis == "xln" or count > 4 or k in (1, count - 1)]
+
+
+def split(value, dim, size):
+    return [lax.slice_in_dim(value, at, at + size, axis=dim) for at in range(0, value.shape[dim], size)]
+
+
+def ahead(value, dim):
+    size = (8, 128)[dim]
+    parts = split(value, dim, size)
+    turned = [pltpu.roll(part, size - 1, dim) for part in parts]
+    edge = lax.broadcasted_iota(jnp.int32, parts[0].shape, dim) == size - 1
+    after = turned[1:] + [parts[-1]]
+    return jnp.concatenate([jnp.where(edge, a, t) for a, t in zip(after, turned)], axis=dim)
+
+
+def behind(value, dim):
+    size = (8, 128)[dim]
+    turned = [pltpu.roll(part, 1, dim) for part in split(value, dim, size)]
+    edge = lax.broadcasted_iota(jnp.int32, turned[0].shape, dim) == 0
+    before = [jnp.zeros_like(turned[0])] + turned[:-1]
+    return jnp.concatenate([jnp.where(edge, a, t) for a, t in zip(before, turned)], axis=dim)
 
 
 def kernel(
@@ -55,12 +80,12 @@
 
     barrier = pltpu.get_barrier_semaphore()
     for axis, me, count in (("inl", my_i, ni_dev), ("xln", my_x, nx_dev)):
-        for k in range(1, count):
+        for k in greeted(axis, count):
             pl.semaphore_signal(
                 barrier, inc=1, device_id={axis: lax.rem(me + k, count)},
                 device_id_type=pl.DeviceIdType.MESH,
             )
-    pl.semaphore_wait(barrier, ni_dev + nx_dev - 2)
+    pl.semaphore_wait(barrier, len(greeted("inl", ni_dev)) + len(greeted("xln", nx_dev)))
 
     sent = []
 
@@ -112,11 +137,6 @@
     bx_last[...] = b[1:end, nx - 1, :]
     got_bx_prev = send(4, bx_last, bx_prev, "xln", True)
 
-    row = lax.broadcasted_iota(jnp.int32, (nx, nz), 0)
-    lane = lax.broadcasted_iota(jnp.int32, (nx, nz), 1)
-    first_row, last_row = row == 0, row == nx - 1
-    first_lane, last_lane = lane == 0, lane == nz - 1
-
     step[...] = jnp.zeros_like(step)
 
     def squares(oi, ox, oz):
@@ -125,14 +145,14 @@
     def pass_one(i, d1):
         here, limit = n[i + 1], b[i + 1]
         di = clip(SIGMA * (n[i + 2] - here), limit)
-        dx = clip(SIGMA * jnp.where(last_row, 0.0, pltpu.roll(here, nx - 1, 0) - here), limit)
-        dz = clip(SIGMA * jnp.where(last_lane, 0.0, pltpu.roll(here, nz - 1, 1) - here), limit)
+        dx = clip(SIGMA * (ahead(here, 0) - here), limit)
+        dz = clip(SIGMA * (ahead(here, 1) - here), limit)
         dual[0, i] = di
         dual[1, i] = dx
         dual[2, i] = dz
         div = di - step[...]
-        div = div + (dx - jnp.where(first_row, 0.0, pltpu.roll(dx, 1, 0)))
-        div = div + (dz - jnp.where(first_lane, 0.0, pltpu.roll(dz, 1, 1)))
+        div = div + (dx - behind(dx, 0))
+        div = div + (dz - behind(dz, 1))
         step[...] = di
         v[i + 1] = here + (2.0 * GAIN) * div
         return d1 + squares(di, dx, dz)
@@ -140,12 +160,12 @@
     zero = jnp.zeros((8, 128), jnp.float32)
     d1 = lax.fori_loop(0, ni - 1, pass_one, zero)
     here, limit = n[top], b[top]
-    dx = clip(SIGMA * jnp.where(last_row, 0.0, pltpu.roll(here, nx - 1, 0) - here), limit)
-    dz = clip(SIGMA * jnp.where(last_lane, 0.0, pltpu.roll(here, nz - 1, 1) - here), limit)
+    dx = clip(SIGMA * (ahead(here, 0) - here), limit)
+    dz = clip(SIGMA * (ahead(here, 1) - here), limit)
     dual[1, ni - 1] = dx
     dual[2, ni - 1] = dz
-    div = (dx - jnp.where(first_row, 0.0, pltpu.roll(dx, 1, 0))) - step[...]
-    div = div + (dz - jnp.where(first_lane, 0.0, pltpu.roll(dz, 1, 1)))
+    div = (dx - behind(dx, 0)) - step[...]
+    div = div + (dz - behind(dz, 1))
     v[top] = here + (2.0 * GAIN) * div
     d1 = d1 + fold(dx * dx + dz * dz)
 
@@ -177,28 +197,32 @@
     got_vx_next = send(9, vx_first, vx_next, "xln", False)
     d1 = d1 + fold(di_last * di_last) + fold(dx_last * dx_last)
 
-    face_row = first_row | last_row
+    row = lax.broadcasted_iota(jnp.int32, (8, nz), 0)
+
+    def inner_rows(value):
+        parts = split(value, 0, 8)
+        parts[0] = jnp.where(row == 0, 0.0, parts[0])
+        parts[-1] = jnp.where(row == 7, 0.0, parts[-1])
+        return jnp.concatenate(parts, axis=0)
 
     def pass_two(i, sums):
         p1, p2, d2 = sums
         here, limit, base = v[i + 1], b[i + 1], n[i + 1]
         oi, ox, oz = dual[0, i], dual[1, i], dual[2, i]
         di = clip(oi + SIGMA * (v[i + 2] - here), limit)
-        ahead = jnp.where(last_row, 0.0, pltpu.roll(here, nx - 1, 0) - here)
-        dx = clip(ox + SIGMA * ahead, limit)
-        ahead = jnp.where(last_lane, 0.0, pltpu.roll(here, nz - 1, 1) - here)
-        dz = clip(oz + SIGMA * ahead, limit)
+        dx = clip(ox + SIGMA * (ahead(here, 0) - here), limit)
+        dz = clip(oz + SIGMA * (ahead(here, 1) - here), limit)
         dual[0, i] = di
         dual[1, i] = dx
         dual[2, i] = dz
         div = di - step[...]
-        div = div + (dx - jnp.where(first_row, 0.0, pltpu.roll(dx, 1, 0)))
-        div = div + (dz - jnp.where(first_lane, 0.0, pltpu.roll(dz, 1, 1)))
+        div = div + (dx - behind(dx, 0))
+        div = div + (dz - behind(dz, 1))
         step[...] = di
         half = 0.5 * (here - base)
         change = GAIN * (div - half)
         out[i] = base + half + change
-        inner = jnp.where(face_row, 0.0, change)
+        inner = inner_rows(change)
         return (
             p1 + fold(half * half),
             p2 + fold(inner * inner),

time: 29.6 us -> 29.2 us (0.986)
  Pallas kernels: 28.9 us -> 28.4 us
    pallas_call x1, Pallas kernels: 25.5 us -> 25 us  [per_device(): pl.pallas_call(functools.partial(kernel, ni_dev, nx_dev), out_shape=(pltp...]
where the time goes in v4:
time: 29.2 us; the launch traced here: 29 us
  Pallas kernels  28.4 us (97%)
  between operations  0.64 us (2%)
    pallas_call x1, Pallas kernels, per_device(): pl.pallas_call(functools.partial(kernel, ni_dev, nx_dev), out_shape=(pltp...  25 us
    pallas_call x1, Pallas kernels, per_device(): pl.pallas_call(put_out, out_shape=(jax.ShapeDtypeStruct((ni, nx, nz), f32...  3.38 us

profile of v4, /device:TPU:0, one launch (start us, length us, event | category | flops | bytes accessed | tf_op | source)
XLA Modules:
  0.0 29.0 jit_solution(9438701532192778743)
XLA Ops:
  0.6 25.0 %denoise.1 = (f32[32,32,512]{2,1,0:T(8,128)S(1)}, f32[3,32,32,512]{3,2,1,0:T(8,128)S(1)}, f32[2,2]{1,0:T(2,128)S(1)}) custom-call(f32[32,32,512]{2,1,0:T(8,128)} %noisy.1, f32[32,32,512]{2,1,0:T(8,128)} %bound.1), custom_call_target="tpu_custom_call" | custom-call | flops 41943040 | bytes 12582912 | tf_op jit(solution)/shard_map/denoise/pallas_call | solution.py:320
  25.7 3.4 %put_out.1 = (f32[32,32,512]{2,1,0:T(8,128)}, f32[3,32,32,512]{3,2,1,0:T(8,128)}, f32[2,2]{1,0:T(2,128)}) custom-call(f32[32,32,512]{2,1,0:T(8,128)S(1)} %get-tuple-element.6.out_held, f32[3,32,32,512]{3,2,1,0:T(8,128)S(1)} %get-tuple-element.7.dual_held, f32[2,2]{1,0:T(2,128)S(1)} %get-tuple-element.8.norms_held), custom_call_target="tpu_custom_call" | custom-call | bytes 8388608 | tf_op jit(solution)/shard_map/put_out/pallas_call | solution.py:356

commit v5 on v4

--- a/solution.py
+++ b/solution.py
@@ -293,16 +293,16 @@
 
 
 def put_out(out_held, dual_held, norms_held, out, dual, norms, sems):
-    half = out.shape[0] // 2
+    size = out.shape[0] // 4
     pairs = [(norms_held, norms)]
-    for at in (0, half):
-        part = pl.ds(at, half)
+    for at in range(0, out.shape[0], size):
+        part = pl.ds(at, size)
         pairs.append((out_held.at[part], out.at[part]))
         for axis in range(3):
             pairs.append((dual_held.at[axis, part], dual.at[axis, part]))
     copies = [pltpu.make_async_copy(src, dst, sems.at[k]) for k, (src, dst) in enumerate(pairs)]
-    for copy in copies:
-        copy.start()
+    for k, copy in enumerate(copies):
+        copy.start(priority=k % 2)
     for copy in copies:
         copy.wait()
 
@@ -362,7 +362,7 @@
         ),
         in_specs=[in_vmem] * 3,
         out_specs=(in_hbm,) * 3,
-        scratch_shapes=[dma((9,))],
+        scratch_shapes=[dma((17,))],
         compiler_params=pltpu.CompilerParams(vmem_limit_bytes=1024 * 1024),
         cost_estimate=pl.CostEstimate(flops=0, bytes_accessed=4 * volume, transcendentals=0),
         name="put_out",

time: 29.2 us -> 29.2 us (level)
  no operation moved by 1% of the time
where the time goes in v5:
time: 29.2 us; the launch traced here: 29.1 us
  Pallas kernels  28.5 us (98%)
  between operations  0.64 us (2%)
    pallas_call x1, Pallas kernels, per_device(): pl.pallas_call(functools.partial(kernel, ni_dev, nx_dev), out_shape=(pltp...  25 us
    pallas_call x1, Pallas kernels, per_device(): pl.pallas_call(put_out, out_shape=(jax.ShapeDtypeStruct((ni, nx, nz), f32...  3.43 us

profile of v5, /device:TPU:0, one launch (start us, length us, event | category | flops | bytes accessed | tf_op | source)
XLA Modules:
  0.0 29.1 jit_solution(10981068713863448618)
XLA Ops:
  0.6 25.0 %denoise.1 = (f32[32,32,512]{2,1,0:T(8,128)S(1)}, f32[3,32,32,512]{3,2,1,0:T(8,128)S(1)}, f32[2,2]{1,0:T(2,128)S(1)}) custom-call(f32[32,32,512]{2,1,0:T(8,128)} %noisy.1, f32[32,32,512]{2,1,0:T(8,128)} %bound.1), custom_call_target="tpu_custom_call" | custom-call | flops 41943040 | bytes 12582912 | tf_op jit(solution)/shard_map/denoise/pallas_call | solution.py:320
  25.7 3.4 %put_out.1 = (f32[32,32,512]{2,1,0:T(8,128)}, f32[3,32,32,512]{3,2,1,0:T(8,128)}, f32[2,2]{1,0:T(2,128)}) custom-call(f32[32,32,512]{2,1,0:T(8,128)S(1)} %get-tuple-element.6.out_held, f32[3,32,32,512]{3,2,1,0:T(8,128)S(1)} %get-tuple-element.7.dual_held, f32[2,2]{1,0:T(2,128)S(1)} %get-tuple-element.8.norms_held), custom_call_target="tpu_custom_call" | custom-call | bytes 8388608 | tf_op jit(solution)/shard_map/put_out/pallas_call | solution.py:356
